TPU v7x, 32 devices: a whole 2x2x4 slice. The times are simulated.
32 devices in a mesh: seq: 16 (over z, y, x), tp: 2 (over core).
Axes of the slice: x: 2, y: 2, z: 4, core: 2. Of those that a mesh axis runs over, the one named last changes fastest.
Arguments:
- query_rows: bfloat16 [2048, 2048], P('seq', 'tp'), may hold values from -350 to 350
- key_rows: bfloat16 [2048, 512], P('seq', 'tp'), may hold values from -6 to 6
- stored_value_rows: bfloat16 [2048, 512], P('seq', 'tp'), may hold values from -6 to 6
- output_grad: bfloat16 [2048, 2048], P('seq', 'tp'), may hold values from -96 to 96
- layer_input: bfloat16 [2048, 4096], P('seq', 'tp'), may hold values from -6 to 6
- key_matrix: bfloat16 [4096, 512], P(None, 'tp'), may hold values from -0.09375 to 0.09375
- value_matrix: bfloat16 [4096, 512], P(None, 'tp'), may hold values from -0.09375 to 0.09375
- run_placement: int32 [16, 16], replicated, may hold values from 0 to 15, as said below
Outputs:
- query_grad: bfloat16 [2048, 2048], P('seq', 'tp')
- input_grad: bfloat16 [2048, 4096], P('seq', 'tp')
- key_weight_grad: float32 [4096, 512], P('seq', 'tp')
- value_weight_grad: float32 [4096, 512], P('seq', 'tp')
Inputs may be any that keep to these rules, and one draw needn't show every extreme that they name: `run_placement`: row j gives, for each storing index d of seq, the slot within sequence block j of the 8 consecutive positions that d holds; every row is a permutation of 0 to 15.
All inputs are finite; a program needn't handle non-finite values.
Results may differ from a plain program's by a relative error of at most 0.0081.
Values may be sent and summed in bfloat16 or wider, within the bound.
A program may use at most 128 MiB of HBM per device.

v0:
```python
import functools
import math

import jax
import jax.numpy as jnp
from jax import lax
from jax.experimental import pallas as pl
from jax.experimental.pallas import tpu as pltpu
from jax.sharding import PartitionSpec as P

HEAD_SIZE = 128
WINDOW_LENGTH = 4096
GROUP = 4
CHUNK = 256
MASKED = -1e30
NT = (((1,), (1,)), ((), ()))
NN = (((1,), (0,)), ((), ()))
TN = (((0,), (0,)), ((), ()))


def dot(a, b, dims):
    return lax.dot_general(a, b, dims, preferred_element_type=jnp.float32)


def attention_kernel(kv_local, q_ref, g_ref, kv_ref, qpos_ref, kpos_ref, dq_ref, dkv_ref, s_ref):
    rows = q_ref.shape[0]
    keys = kv_ref.shape[0]
    kv_width = kv_local * HEAD_SIZE
    wide = GROUP * rows
    chunks = keys // CHUNK
    scale = 1.0 / math.sqrt(HEAD_SIZE)
    qpos = jnp.concatenate([qpos_ref[...]] * GROUP, axis=1)
    for c in range(kv_local):
        first = c * GROUP
        heads = [slice((first + i) * HEAD_SIZE, (first + i + 1) * HEAD_SIZE) for i in range(GROUP)]
        q4 = jnp.concatenate([q_ref[:, h] for h in heads], axis=0)
        g4 = jnp.concatenate([g_ref[:, h] for h in heads], axis=0)
        k_cols = slice(c * HEAD_SIZE, (c + 1) * HEAD_SIZE)
        v_cols = slice(kv_width + c * HEAD_SIZE, kv_width + (c + 1) * HEAD_SIZE)

        def forward(i, carry):
            top, total, weighted = carry
            at = pl.ds(pl.multiple_of(i * CHUNK, CHUNK), CHUNK)
            kpos = kpos_ref[at, :]
            seen = (kpos <= qpos) & (kpos > qpos - WINDOW_LENGTH)
            s = jnp.where(seen, dot(kv_ref[at, k_cols], q4, NT) * scale, MASKED)
            dp = dot(kv_ref[at, v_cols], g4, NT)
            s_ref[at, :] = s
            new_top = jnp.maximum(top, jnp.max(s, axis=0, keepdims=True))
            e = jnp.exp(s - new_top)
            factor = jnp.exp(top - new_top)
            total = total * factor + jnp.sum(e, axis=0, keepdims=True)
            weighted = weighted * factor + jnp.sum(e * dp, axis=0, keepdims=True)
            return new_top, total, weighted

        zero = jnp.zeros((1, wide), jnp.float32)
        top, total, weighted = lax.fori_loop(
            0, chunks, forward, (jnp.full((1, wide), MASKED, jnp.float32), zero, zero)
        )
        lse = top + jnp.log(total)
        delta = weighted / total

        def backward(i, acc):
            at = pl.ds(pl.multiple_of(i * CHUNK, CHUNK), CHUNK)
            prob = jnp.exp(s_ref[at, :] - lse)
            dp = dot(kv_ref[at, v_cols], g4, NT)
            ds = (prob * (dp - delta)).astype(jnp.bfloat16)
            dkv_ref[at, k_cols] = (dot(ds, q4, NN) * scale).astype(dkv_ref.dtype)
            dkv_ref[at, v_cols] = dot(prob.astype(jnp.bfloat16), g4, NN).astype(dkv_ref.dtype)
            return acc + dot(kv_ref[at, k_cols], ds, TN)

        acc = lax.fori_loop(0, chunks, backward, jnp.zeros((HEAD_SIZE, wide), jnp.float32))
        dq = (jnp.transpose(acc) * scale).astype(jnp.bfloat16)
        for i, h in enumerate(heads):
            dq_ref[:, h] = dq[i * rows : (i + 1) * rows]


def attention(q, g, kv, qpos, kpos, grad_type):
    rows, width = q.shape
    keys, kv_cols = kv.shape
    wide = GROUP * rows
    vmem = pl.BlockSpec(memory_space=pltpu.VMEM)
    return pl.pallas_call(
        functools.partial(attention_kernel, kv_cols // (2 * HEAD_SIZE)),
        out_shape=(
            jax.ShapeDtypeStruct((rows, width), jnp.bfloat16),
            jax.ShapeDtypeStruct((keys, kv_cols), grad_type),
        ),
        in_specs=[vmem] * 5,
        out_specs=(vmem, vmem),
        scratch_shapes=[pltpu.VMEM((keys, wide), jnp.float32)],
        compiler_params=pltpu.CompilerParams(vmem_limit_bytes=60 * 2**20),
    )(q, g, kv, qpos, kpos)


def positions(run_placement, rows_here):
    seq_count = run_placement.shape[0]
    run_rows = rows_here // seq_count
    block = jnp.arange(seq_count, dtype=jnp.int32)[:, None] * rows_here
    start = jnp.transpose(block + run_placement * run_rows)
    return start[:, :, None] + jnp.arange(run_rows, dtype=jnp.int32)


def local(
    query_rows,
    key_rows,
    stored_value_rows,
    output_grad,
    layer_input,
    key_matrix,
    value_matrix,
    run_placement,
):
    seq_index = lax.axis_index("seq")
    rows_here = query_rows.shape[0]
    kv_width = key_rows.shape[1]
    pos = positions(run_placement, rows_here)
    kpos = pos.reshape(-1, 1)
    qpos = lax.dynamic_index_in_dim(pos, seq_index, 0, keepdims=False).reshape(1, rows_here)
    own_kv = jnp.concatenate([key_rows, stored_value_rows], axis=1)
    kv_all = lax.all_gather(own_kv, "seq", axis=0, tiled=True)
    full_input = lax.all_gather(layer_input, "tp", axis=1, tiled=True)
    input_columns = lax.all_to_all(full_input, "seq", split_axis=1, concat_axis=0, tiled=True)
    query_grad, partial_kv = attention(query_rows, output_grad, kv_all, qpos, kpos, jnp.float32)
    kv_grad = lax.psum_scatter(partial_kv, "seq", scatter_dimension=0, tiled=True).astype(jnp.bfloat16)
    partial_input = dot(kv_grad[:, :kv_width], key_matrix, NT) + dot(
        kv_grad[:, kv_width:], value_matrix, NT
    )
    input_grad = lax.psum_scatter(partial_input, "tp", scatter_dimension=1, tiled=True).astype(
        jnp.bfloat16
    )
    weight_rows = dot(input_columns, lax.all_gather(kv_grad, "seq", axis=0, tiled=True), TN)
    return (query_grad, input_grad, weight_rows[:, :kv_width], weight_rows[:, kv_width:])


def solution(mesh):
    placed = (P("seq", "tp"),) * 5 + (P(None, "tp"), P(None, "tp"), P())
    return jax.shard_map(
        local,
        mesh=mesh,
        in_specs=placed,
        out_specs=(P("seq", "tp"),) * 4,
        check_vma=False,
    )
```

profile of v0, /device:TPU:0, one launch (start us, length us, event | category | flops | bytes accessed | tf_op | source)
XLA Modules:
  0.0 272.3 jit_solution(4364122269060168016)
XLA Ops:
  8.0 0.0 copy-start
  8.0 0.0 all-gather.4.cloned.1.call-start
  8.1 1.7 pad_maximum_fusion
  9.7 0.0 all-gather.4.cloned.1.call-update
  9.8 0.0 reduce-scatter.3.cloned.1.call-start
  9.8 0.8 add_bitcast_fusion
  10.6 0.1 copy.19
  10.7 0.1 iota_add_fusion
  10.8 1.3 add.50.kpos_ref
  12.1 0.6 reshape.44.qpos_ref
  12.7 62.6 %all-gather.4.cloned.1.call-done.kv_ref = bf16[2048,512]{1,0:T(8,128)(2,1)} async-done(((bf16[128,512]{1,0:T(8,128)(2,1)}), bf16[2048,512]{1,0:T(8,128)(2,1)}) %all-gather.4.cloned.1.call-update) | async-done | bytes 2097168 | tf_op jit(solution)/shard_map/all_gather | solution.py:121
  75.3 18.1 %shard_map.111 = (bf16[128,1024]{1,0:T(8,128)(2,1)}, f32[2048,512]{1,0:T(8,128)}) custom-call(bf16[128,1024]{1,0:T(8,128)(2,1)} %q_ref.1, bf16[128,1024]{1,0:T(8,128)(2,1)} %g_ref.1, bf16[2048,512]{1,0:T(8,128)(2,1)} %all-gather.4.cloned.1.call-done.kv_ref, s32[1,128]{1,0:T(1,128)} %reshape.44.qpos_ref, s32[2048,1]{1,0:T(8,128)} %add.50.kpos_ref), custom_call_target="tpu_custom_call" | custom-call | tf_op jit(solution)/shard_map/pallas_call | solution.py:83
  93.4 0.0 copy-start.3
  93.4 0.0 reduce-scatter.3.cloned.1.call-update
  93.5 0.0 all-gather.8.cloned.1.call-start
  93.5 1.0 copy-done.3
  94.5 1.0 copy.21
  95.5 0.0 all-gather.8.cloned.1.call-update
  95.5 0.0 all-gather.6.cloned.1.call-start
  95.5 92.1 %reduce-scatter.3.cloned.1.call-done = f32[128,512]{1,0:T(8,128)} async-done(((f32[2048,512]{1,0:T(8,128)}), f32[128,512]{1,0:T(8,128)}) %reduce-scatter.3.cloned.1.call-update) | async-done | bytes 262160 | tf_op jit(solution)/shard_map/reduce_scatter | solution.py:125
  187.7 1.6 convert_element_type.6
  189.3 0.0 all-gather.6.cloned.1.call-update
  189.3 0.0 copy-start.2
  189.3 0.0 reduce-scatter.5.cloned.1.call-start
  189.4 0.0 copy-done
  189.4 0.0 copy-start.1
  189.4 1.8 fusion.1
  191.2 0.0 copy-done.2
  191.2 0.0 copy-done.1
  191.2 2.1 convolution_add_fusion
  193.4 0.0 reduce-scatter.5.cloned.1.call-update
  193.4 0.0 all-gather.8.cloned.1.call-done
  193.4 39.2 %all_to_all.19 = bf16[128,16,256]{0,2,1:T(8,128)(2,1)} all-to-all(bf16[128,16,256]{0,2,1:T(8,128)(2,1)} %bitcast.13), channel_id=1, replica_groups=mesh['seq'=16,'tp'=2] {'seq'}, dimensions={1} | all-to-all | bytes 2097152 | tf_op jit(solution)/shard_map/all_to_all | solution.py:123
  232.6 1.5 copy.22
  234.1 18.1 %all-gather.6.cloned.1.call-done = bf16[2048,512]{1,0:T(8,128)(2,1)} async-done(((bf16[128,512]{1,0:T(8,128)(2,1)}), bf16[2048,512]{1,0:T(8,128)(2,1)}) %all-gather.6.cloned.1.call-update) | async-done | bytes 2097168 | tf_op jit(solution)/shard_map/all_gather | solution.py:132
  252.2 2.3 convolution_bitcast_fusion
  254.6 0.8 copy.23
  255.4 0.8 copy.24
  256.2 6.4 %reduce-scatter.5.cloned.1.call-done = f32[128,2048]{1,0:T(8,128)} async-done(((f32[128,4096]{1,0:T(8,128)}), f32[128,2048]{1,0:T(8,128)}) %reduce-scatter.5.cloned.1.call-update) | async-done | bytes 1048592 | tf_op jit(solution)/shard_map/reduce_scatter | solution.py:129
  262.7 2.1 convert_element_type.7
  (3 shorter events, 0.0 us)
Async XLA Ops:
  8.0 181.4 %copy-start = (bf16[4096,256]{1,0:T(8,128)(2,1)S(1)}, bf16[4096,256]{1,0:T(8,128)(2,1)}, u32[]{:S(2)}) copy-start(bf16[4096,256]{1,0:T(8,128)(2,1)} %param.13) | copy-start | bytes 6291460
  8.0 67.3 %all-gather.4.cloned.1.call-start = ((), (), s32[]{:S(2)}) async-start(), calls=%async_computation.3 | async-start | bytes 2228224 | tf_op jit(solution)/shard_map/all_gather | solution.py:121
  9.8 177.9 %reduce-scatter.3.cloned.1.call-start = ((), (), s32[]{:S(2)}) async-start(), calls=%async_computation.4 | async-start | bytes 4456448 | tf_op jit(solution)/shard_map/reduce_scatter | solution.py:125
  93.4 1.0 copy-start.3
  93.5 100.0 %all-gather.8.cloned.1.call-start = ((), (), s32[]{:S(2)}) async-start(), calls=%async_computation.7 | async-start | bytes 1572864 | tf_op jit(solution)/shard_map/all_gather | solution.py:122
  95.5 156.7 %all-gather.6.cloned.1.call-start = ((), (), s32[]{:S(2)}) async-start(), calls=%async_computation.6 | async-start | bytes 2228224 | tf_op jit(solution)/shard_map/all_gather | solution.py:132
  189.3 1.9 copy-start.2
  189.3 73.3 %reduce-scatter.5.cloned.1.call-start = ((), (), s32[]{:S(2)}) async-start(), calls=%async_computation.5 | async-start | bytes 3145728 | tf_op jit(solution)/shard_map/reduce_scatter | solution.py:129
  189.4 1.8 copy-start.1
Sparse Core Ops, SparseCore 0:
  12.2 63.0 all-gather.3
  93.6 94.0 reduce-scatter.2
Sparse Core Ops, SparseCore 1:
  96.1 7.7 all-gather.7
  189.4 62.7 all-gather.5
  254.3 8.3 reduce-scatter.4
where the time goes:
time: 273 us; the launch traced here: 272 us
  waiting for transfers between devices  179 us (66%)
  blocking collectives  39.2 us (14%)
  Pallas kernels  18.1 us (7%)
  between operations  15.8 us (6%)
  local copies, waits for them, and re-layouts  7.17 us (3%)
  matrix products  6.27 us (2%)
  other arithmetic  6.25 us (2%)
    reduce_scatter x1, waiting for transfers between devices, local(): lax.psum_scatter(partial_kv, 'seq', scatter_dimension=0, tiled=True)  92.1 us
    all_gather x1, waiting for transfers between devices, local(): kv_all = lax.all_gather(own_kv, 'seq', axis=0, tiled=True)  62.6 us
    all_to_all x1, blocking collectives, local(): lax.all_to_all(full_input, 'seq', split_axis=1, concat_axis=0, tiled=True)  39.2 us
    pallas_call x1, Pallas kernels, attention(): pl.pallas_call(functools.partial(attention_kernel, kv_cols // (2 * HEAD_S...  18.1 us
    all_gather x1, waiting for transfers between devices, local(): lax.all_gather(kv_grad, 'seq', axis=0, tiled=True)  18.1 us
    reduce_scatter x1, waiting for transfers between devices, local(): lax.psum_scatter(partial_input, 'tp', scatter_dimension=1, tiled=True)  6.42 us
    dot_general x3, matrix products, dot(): return lax.dot_general(a, b, dims, preferred_element_type=jnp.float32)  6.27 us
  transfers between devices with their start and end apart: 5, of which 4 were waited for; matrix products, arithmetic and copies ran while one was open for 5% of the time, Pallas kernels for 0%

commit v1 on v0

--- a/solution.py
+++ b/solution.py
@@ -1,4 +1,3 @@
-import functools
 import math
 
 import jax
@@ -16,20 +15,169 @@
 NT = (((1,), (1,)), ((), ()))
 NN = (((1,), (0,)), ((), ()))
 TN = (((0,), (0,)), ((), ()))
+MESH = pl.DeviceIdType.MESH
 
 
 def dot(a, b, dims):
     return lax.dot_general(a, b, dims, preferred_element_type=jnp.float32)
 
 
-def attention_kernel(kv_local, q_ref, g_ref, kv_ref, qpos_ref, kpos_ref, dq_ref, dkv_ref, s_ref):
+def flip(index, bit):
+    return index + bit - 2 * bit * ((index // bit) % 2)
+
+
+def bit_orders(count):
+    bits = []
+    while count > 1:
+        count //= 2
+        bits.append(count)
+    return (bits[:-2] + bits[-2:][::-1], bits)
+
+
+def step_kernel(
+    q_ref, g_ref, k_ref, v_ref, qpos_ref, kpos_ref, x_ref, km_ref, vm_ref,
+    dq_ref, all_ref, pair_ref, cols_ref, km_out, vm_out,
+    kv_ref, part_ref, land_ref, s_ref,
+    send_sem, recv_sem, x_send, x_recv, side_send, side_recv, local_sem,
+):
+    n = lax.axis_size("seq")
+    me = lax.axis_index("seq")
+    tp = lax.axis_index("tp")
     rows = q_ref.shape[0]
     keys = kv_ref.shape[0]
-    kv_width = kv_local * HEAD_SIZE
+    kv_width = k_ref.shape[1]
+    kv_local = kv_width // HEAD_SIZE
+    features = x_ref.shape[1]
+    half = n // 2
+    x_width = cols_ref.shape[1]
+    block_width = features // half
+    orders = bit_orders(n)
+    stages = len(orders[0])
+    scale = 1.0 / math.sqrt(HEAD_SIZE)
+    other = {"seq": me, "tp": 1 - tp}
+    groups = []
+    for c in range(kv_local):
+        groups.append((slice(c * HEAD_SIZE, (c + 1) * HEAD_SIZE), orders[0]))
+        groups.append((slice(kv_width + c * HEAD_SIZE, kv_width + (c + 1) * HEAD_SIZE), orders[1]))
+
+    barrier = pltpu.get_barrier_semaphore()
+    for step in range(1, n):
+        pl.semaphore_signal(
+            barrier, inc=1, device_id={"seq": (me + step) % n, "tp": tp}, device_id_type=MESH
+        )
+    pl.semaphore_signal(barrier, inc=1, device_id=other, device_id_type=MESH)
+    pl.semaphore_wait(barrier, n)
+
+    def block_of(order, ident):
+        index = me
+        for stage, bit in enumerate(order):
+            if (ident >> stage) & 1:
+                index = flip(index, bit)
+        return index
+
+    def span(index):
+        return pl.ds(pl.multiple_of(index * rows, rows), rows)
+
+    sent = []
+
+    def send(phase, g, stage, ident, src, dst):
+        copy = pltpu.make_async_remote_copy(
+            src_ref=src,
+            dst_ref=dst,
+            send_sem=send_sem.at[phase, g, 2**stage + ident],
+            recv_sem=recv_sem.at[phase, g, 2**stage + ident],
+            device_id={"seq": flip(me, groups[g][1][stage]), "tp": tp},
+            device_id_type=MESH,
+        )
+        copy.start()
+        sent.append(copy)
+        return copy
+
+    def gather(phase, buffer, own):
+        flying = {}
+
+        def forward(g, ident, first):
+            cols, order = groups[g]
+            place = buffer.at[span(block_of(order, ident)), cols]
+            src = own(g) if ident == 0 else place
+            for stage in range(first, stages):
+                flying[g, stage, ident] = send(phase, g, stage, ident, src, place)
+
+        for g in range(len(groups)):
+            forward(g, 0, 0)
+        for stage in range(stages):
+            for ident in range(2**stage):
+                for g in range(len(groups)):
+                    flying[g, stage, ident].wait_recv()
+                    forward(g, 2**stage + ident, stage + 1)
+
+    def own_input(g):
+        cols = groups[g][0]
+        if cols.start < kv_width:
+            return k_ref.at[:, cols]
+        return v_ref.at[:, slice(cols.start - kv_width, cols.stop - kv_width)]
+
+    kv_ref[span(me), :kv_width] = k_ref[...]
+    kv_ref[span(me), kv_width:] = v_ref[...]
+    gather(0, kv_ref, own_input)
+
+    side = []
+    for i, (src, dst) in enumerate(((km_ref, km_out), (vm_ref, vm_out))):
+        copy = pltpu.make_async_remote_copy(
+            src_ref=src.at[pl.ds(pl.multiple_of((1 - tp) * features, features), features), :],
+            dst_ref=dst,
+            send_sem=side_send.at[i],
+            recv_sem=side_recv.at[i],
+            device_id=other,
+            device_id_type=MESH,
+        )
+        copy.start()
+        side.append(copy)
+
+    def columns_of(target):
+        start = ((target % half) * block_width) // x_width * x_width
+        return x_ref.at[:, pl.ds(pl.multiple_of(start, x_width), x_width)]
+
+    def x_copy(target, slot, source):
+        return pltpu.make_async_remote_copy(
+            src_ref=columns_of(target),
+            dst_ref=cols_ref.at[span(me), :],
+            send_sem=x_send.at[slot],
+            recv_sem=x_recv.at[source],
+            device_id={"seq": target, "tp": tp},
+            device_id_type=MESH,
+        )
+
+    holder = tp == me // half
+    own_columns = pltpu.make_async_copy(columns_of(me), cols_ref.at[span(me), :], local_sem)
+
+    @pl.when(holder)
+    def _():
+        own_columns.start()
+
+    for slot in range(half):
+        target = tp * half + (me + slot) % half
+
+        @pl.when(target != me)
+        def _():
+            x_copy(target, slot, me).start()
+
+    qpos = jnp.concatenate([qpos_ref[...]] * GROUP, axis=1)
     wide = GROUP * rows
     chunks = keys // CHUNK
-    scale = 1.0 / math.sqrt(HEAD_SIZE)
-    qpos = jnp.concatenate([qpos_ref[...]] * GROUP, axis=1)
+    moving = {}
+
+    def reduce_send(g, stage, ident):
+        cols, order = groups[g]
+        moving[g, stage, ident] = send(
+            1,
+            g,
+            stage,
+            ident,
+            part_ref.at[span(block_of(order, 2**stage + ident)), cols],
+            land_ref.at[slice((2**stage + ident) * rows, (2**stage + ident + 1) * rows), cols],
+        )
+
     for c in range(kv_local):
         first = c * GROUP
         heads = [slice((first + i) * HEAD_SIZE, (first + i + 1) * HEAD_SIZE) for i in range(GROUP)]
@@ -65,32 +213,128 @@
             prob = jnp.exp(s_ref[at, :] - lse)
             dp = dot(kv_ref[at, v_cols], g4, NT)
             ds = (prob * (dp - delta)).astype(jnp.bfloat16)
-            dkv_ref[at, k_cols] = (dot(ds, q4, NN) * scale).astype(dkv_ref.dtype)
-            dkv_ref[at, v_cols] = dot(prob.astype(jnp.bfloat16), g4, NN).astype(dkv_ref.dtype)
+            part_ref[at, k_cols] = (dot(ds, q4, NN) * scale).astype(jnp.bfloat16)
+            part_ref[at, v_cols] = dot(prob.astype(jnp.bfloat16), g4, NN).astype(jnp.bfloat16)
             return acc + dot(kv_ref[at, k_cols], ds, TN)
 
         acc = lax.fori_loop(0, chunks, backward, jnp.zeros((HEAD_SIZE, wide), jnp.float32))
         dq = (jnp.transpose(acc) * scale).astype(jnp.bfloat16)
         for i, h in enumerate(heads):
             dq_ref[:, h] = dq[i * rows : (i + 1) * rows]
-
-
-def attention(q, g, kv, qpos, kpos, grad_type):
+        for ident in range(2 ** (stages - 1)):
+            for g in (2 * c, 2 * c + 1):
+                reduce_send(g, stages - 1, ident)
+
+    @pl.when(holder)
+    def _():
+        own_columns.wait()
+        for step in range(1, n):
+            x_copy(me, 0, (me + step) % n).wait_recv()
+
+    relay = pltpu.make_async_remote_copy(
+        src_ref=cols_ref,
+        dst_ref=cols_ref,
+        send_sem=side_send.at[2],
+        recv_sem=side_recv.at[2],
+        device_id=other,
+        device_id_type=MESH,
+    )
+
+    @pl.when(holder)
+    def _():
+        relay.start()
+
+    def add(g, stage, ident, out_ref):
+        cols, order = groups[g]
+        moving[g, stage, ident].wait_recv()
+        at = span(block_of(order, ident))
+        slot = 2**stage + ident
+        landed = land_ref[slot * rows : (slot + 1) * rows, cols].astype(jnp.float32)
+        out_ref[at, cols] = (part_ref[at, cols].astype(jnp.float32) + landed).astype(jnp.bfloat16)
+
+    for stage in range(stages - 1, 0, -1):
+        middle = 2 ** (stage - 1)
+        for g in range(len(groups)):
+            for ident in range(middle, 2 * middle):
+                add(g, stage, ident, part_ref)
+            for ident in range(middle):
+                reduce_send(g, stage - 1, ident)
+        for g in range(len(groups)):
+            for ident in range(middle):
+                add(g, stage, ident, part_ref)
+    for g in range(len(groups)):
+        add(g, 0, 0, all_ref)
+    mate = pltpu.make_async_remote_copy(
+        src_ref=all_ref.at[span(me), :],
+        dst_ref=pair_ref,
+        send_sem=side_send.at[3],
+        recv_sem=side_recv.at[3],
+        device_id=other,
+        device_id_type=MESH,
+    )
+    mate.start()
+    gather(2, all_ref, lambda g: all_ref.at[span(me), groups[g][0]])
+
+    for copy in sent:
+        copy.wait_send()
+    for copy in side + [mate]:
+        copy.wait()
+    for slot in range(half):
+        target = tp * half + (me + slot) % half
+
+        @pl.when(target != me)
+        def _():
+            x_copy(target, slot, me).wait_send()
+
+    @pl.when(holder)
+    def _():
+        relay.wait_send()
+
+    @pl.when(tp != me // half)
+    def _():
+        relay.wait_recv()
+
+
+def step(n, q, g, k, v, qpos, kpos, x, km, vm):
     rows, width = q.shape
-    keys, kv_cols = kv.shape
-    wide = GROUP * rows
+    kv_width = k.shape[1]
+    features = x.shape[1]
+    keys = n * rows
+    x_width = max(2 * features // n, 128)
+    groups = 2 * kv_width // HEAD_SIZE
     vmem = pl.BlockSpec(memory_space=pltpu.VMEM)
+    hbm = pl.BlockSpec(memory_space=pl.ANY)
+    kind = jnp.bfloat16
+    dma = pltpu.SemaphoreType.DMA
     return pl.pallas_call(
-        functools.partial(attention_kernel, kv_cols // (2 * HEAD_SIZE)),
+        step_kernel,
         out_shape=(
-            jax.ShapeDtypeStruct((rows, width), jnp.bfloat16),
-            jax.ShapeDtypeStruct((keys, kv_cols), grad_type),
+            jax.ShapeDtypeStruct((rows, width), kind),
+            jax.ShapeDtypeStruct((keys, 2 * kv_width), kind),
+            jax.ShapeDtypeStruct((rows, 2 * kv_width), kind),
+            jax.ShapeDtypeStruct((keys, x_width), kind),
+            jax.ShapeDtypeStruct((features, kv_width), kind),
+            jax.ShapeDtypeStruct((features, kv_width), kind),
         ),
-        in_specs=[vmem] * 5,
-        out_specs=(vmem, vmem),
-        scratch_shapes=[pltpu.VMEM((keys, wide), jnp.float32)],
-        compiler_params=pltpu.CompilerParams(vmem_limit_bytes=60 * 2**20),
-    )(q, g, kv, qpos, kpos)
+        in_specs=[vmem] * 6 + [hbm] * 3,
+        out_specs=(vmem, vmem, vmem, hbm, hbm, hbm),
+        scratch_shapes=[
+            pltpu.VMEM((keys, 2 * kv_width), kind),
+            pltpu.VMEM((keys, 2 * kv_width), kind),
+            pltpu.VMEM((keys, 2 * kv_width), kind),
+            pltpu.VMEM((keys, GROUP * rows), jnp.float32),
+            dma((3, groups, n)),
+            dma((3, groups, n)),
+            dma((n // 2,)),
+            dma((n,)),
+            dma((4,)),
+            dma((4,)),
+            dma,
+        ],
+        compiler_params=pltpu.CompilerParams(
+            vmem_limit_bytes=63 * 2**20, collective_id=0, has_side_effects=True
+        ),
+    )(q, g, k, v, qpos, kpos, x, km, vm)
 
 
 def positions(run_placement, rows_here):
@@ -117,20 +361,36 @@
     pos = positions(run_placement, rows_here)
     kpos = pos.reshape(-1, 1)
     qpos = lax.dynamic_index_in_dim(pos, seq_index, 0, keepdims=False).reshape(1, rows_here)
-    own_kv = jnp.concatenate([key_rows, stored_value_rows], axis=1)
-    kv_all = lax.all_gather(own_kv, "seq", axis=0, tiled=True)
-    full_input = lax.all_gather(layer_input, "tp", axis=1, tiled=True)
-    input_columns = lax.all_to_all(full_input, "seq", split_axis=1, concat_axis=0, tiled=True)
-    query_grad, partial_kv = attention(query_rows, output_grad, kv_all, qpos, kpos, jnp.float32)
-    kv_grad = lax.psum_scatter(partial_kv, "seq", scatter_dimension=0, tiled=True).astype(jnp.bfloat16)
-    partial_input = dot(kv_grad[:, :kv_width], key_matrix, NT) + dot(
-        kv_grad[:, kv_width:], value_matrix, NT
+    seq_count = run_placement.shape[0]
+    query_grad, kv_all, kv_mate, columns, key_far, value_far = step(
+        seq_count,
+        query_rows,
+        output_grad,
+        key_rows,
+        stored_value_rows,
+        qpos,
+        kpos,
+        layer_input,
+        key_matrix,
+        value_matrix,
     )
-    input_grad = lax.psum_scatter(partial_input, "tp", scatter_dimension=1, tiled=True).astype(
-        jnp.bfloat16
-    )
-    weight_rows = dot(input_columns, lax.all_gather(kv_grad, "seq", axis=0, tiled=True), TN)
-    return (query_grad, input_grad, weight_rows[:, :kv_width], weight_rows[:, kv_width:])
+    features = layer_input.shape[1]
+    tp_index = lax.axis_index("tp")
+    kv_grad = lax.dynamic_slice_in_dim(kv_all, seq_index * rows_here, rows_here, 0)
+    key_near = lax.dynamic_slice_in_dim(key_matrix, tp_index * features, features, 0)
+    value_near = lax.dynamic_slice_in_dim(value_matrix, tp_index * features, features, 0)
+    input_grad = (
+        dot(kv_grad[:, :kv_width], key_near, NT)
+        + dot(kv_grad[:, kv_width:], value_near, NT)
+        + dot(kv_mate[:, :kv_width], key_far, NT)
+        + dot(kv_mate[:, kv_width:], value_far, NT)
+    ).astype(jnp.bfloat16)
+    block_width = 2 * features // seq_count
+    shift = (seq_index * block_width) % columns.shape[1]
+    columns = lax.dynamic_slice_in_dim(columns, shift, block_width, 1)
+    key_weight = dot(columns, kv_all[:, :kv_width], TN)
+    value_weight = dot(columns, kv_all[:, kv_width:], TN)
+    return (query_grad, input_grad, key_weight, value_weight)
 
 
 def solution(mesh):

time: 273 us -> 101 us (0.37)
  waiting for transfers between devices: 179 us -> 0 us
  Pallas kernels: 18.1 us -> 88.5 us
  blocking collectives: 39.2 us -> 0 us
  between operations: 15.8 us -> 0.75 us
  other arithmetic: 6.25 us -> 0.87 us
  local copies, waits for them, and re-layouts: 7.17 us -> 3.44 us
    reduce_scatter x2 -> x0, waiting for transfers between devices: 98.5 us -> none  [the longest x1 92.1 us: local(): lax.psum_scatter(partial_kv, 'seq', scatter_dimension=0, tiled=True)]
    all_gather x3 -> x0, waiting for transfers between devices: 80.7 us -> none  [the longest x1 62.6 us: local(): kv_all = lax.all_gather(own_kv, 'seq', axis=0, tiled=True)]
    pallas_call x1, Pallas kernels: 18.1 us -> 88.5 us  [step(): pl.pallas_call(step_kernel, out_shape=(jax.ShapeDtypeStruct((rows, width)...]
    all_to_all x1 -> x0, blocking collectives: 39.2 us -> none  [local(): lax.all_to_all(full_input, 'seq', split_axis=1, concat_axis=0, tiled=True)]
    convert_element_type x2 -> x0, other arithmetic: 3.71 us -> none  [the longest x1 2.08 us: local(): lax.psum_scatter(partial_input, 'tp', scatter_dimension=1, tiled=True)]
    dot_general x3 -> x6, matrix products: 6.27 us -> 7.37 us  [dot(): return lax.dot_general(a, b, dims, preferred_element_type=jnp.float32)]
  transfers between devices with their start and end apart: 5 -> 0, of which waited for: 4 -> 0; matrix products, arithmetic and copies ran while one was open for 5% -> 0% of each run, Pallas kernels for 0% -> 0%
where the time goes in v1:
time: 101 us
  Pallas kernels  88.5 us (88%)
  matrix products  7.37 us (7%)
  local copies, waits for them, and re-layouts  3.44 us (3%)
    pallas_call x1, Pallas kernels, step(): pl.pallas_call(step_kernel, out_shape=(jax.ShapeDtypeStruct((rows, width)...  88.5 us
    dot_general x6, matrix products, dot(): return lax.dot_general(a, b, dims, preferred_element_type=jnp.float32)  7.37 us

profile of v1, /device:TPU:0, one launch (start us, length us, event | category | flops | bytes accessed | tf_op | source)
XLA Modules:
  0.0 101.0 jit_solution(928874106085621939)
XLA Ops:
  0.6 0.8 add_bitcast_fusion
  1.4 0.1 copy.13
  1.5 0.1 iota_add_fusion
  1.6 0.6 reshape.41.qpos_ref
  2.2 1.3 %add.66.kpos_ref = s32[2048,1]{1,0:T(8,128)} reshape(s32[16,16,8]{2,1,0:T(8,128)S(1)} %iota_add_fusion) | data formatting | bytes 16384 | tf_op jit(solution)/shard_map/add | solution.py:345
  3.5 88.5 %shard_map.111 = (bf16[128,1024]{1,0:T(8,128)(2,1)}, bf16[2048,512]{1,0:T(8,128)(2,1)}, bf16[128,512]{1,0:T(8,128)(2,1)}, bf16[2048,256]{1,0:T(8,128)(2,1)}, bf1...) custom-call(bf16[128,1024]{1,0:T(8,128)(2,1)} %q_ref.1, bf16[128,1024]{1,0:T(8,128)(2,1)} %g_ref.1, ...), custom_call_target="tpu_custom_call" | custom-call | tf_op jit(solution)/shard_map/pallas_call | solution.py:309
  92.1 0.0 copy-start
  92.1 1.9 %fusion.6 = f32[128,2048]{1,0:T(8,128)S(1)} fusion(bf16[4096,256]{1,0:T(8,128)(2,1)} %km_ref.1, s32[]{:T(128)S(6)} %select_n.19, bf16[2048,512]{1,0:T(8,128)(2,1)} %get-tuple-element.11, s32[]{:T(128)S(6)} %select_n.18), kind=kOutput, calls=%fused_computation.9 | convolution fusion | flops 134217728 | bytes 2162696 | tf_op jit(solution)/shard_map/dot_general | solution.py:22
  94.0 0.0 copy-start.6
  94.0 0.0 copy-done
  94.0 0.0 copy-start.3
  94.0 1.4 %convolution_add_fusion.2 = f32[128,2048]{1,0:T(8,128)S(1)} fusion(f32[128,2048]{1,0:T(8,128)S(1)} %fusion.6, bf16[4096,256]{1,0:T(8,128)(2,1)S(1)} %copy-done, s32[]{:T(128)S(6)} %select_n.19, bf16[2048,512]{1,0:T(8,128)(2,1)} %get-tuple-element.11, s32[]{:T(128)S(6)} %select_n.18, s32[]{:T(128)S(6)} %add.67), kind=kOutput, calls=%fused_computation.2 | convolution fusion | flops 134479872 | bytes 3211276 | tf_op jit(solution)/shard_map/dot_general | solution.py:22
  95.4 0.0 copy-start.4
  95.4 0.0 copy-done.6
  95.4 0.0 copy-done.3
  95.5 0.0 copy-start.2
  95.5 0.5 convolution_add_fusion.1
  95.9 0.0 copy-start.1
  96.0 0.7 copy-done.4
  96.6 1.3 %fusion = bf16[128,2048]{1,0:T(8,128)(2,1)} fusion(f32[128,2048]{1,0:T(8,128)S(1)} %convolution_add_fusion.1, bf16[2048,256]{1,0:T(8,128)(2,1)S(1)} %copy-done.4, bf16[128,512]{1,0:T(8,128)(2,1)S(1)} %copy-done.6), kind=kOutput, calls=%fused_computation.3 | convolution fusion | flops 134742016 | bytes 2686976 | tf_op jit(solution)/shard_map/dot_general | solution.py:22
  97.9 0.0 copy-done.2
  97.9 0.0 copy-done.1
  97.9 0.0 copy-start.5
  97.9 1.2 %fusion.1 = f32[256,256]{1,0:T(8,128)} fusion(bf16[2048,256]{1,0:T(8,128)(2,1)S(1)} %copy-done.1, bf16[2048,512]{1,0:T(8,128)(2,1)S(1)} %copy-done.2), kind=kOutput, calls=%fused_computation.4 | convolution fusion | flops 268435456 | bytes 2359296 | tf_op jit(solution)/shard_map/dot_general | solution.py:22
  99.1 1.2 %fusion.3 = f32[256,256]{1,0:T(8,128)} fusion(bf16[2048,256]{1,0:T(8,128)(2,1)S(1)} %copy-done.1, bf16[2048,512]{1,0:T(8,128)(2,1)S(1)} %copy-done.2), kind=kOutput, calls=%fused_computation.6 | convolution fusion | flops 268435456 | bytes 2359296 | tf_op jit(solution)/shard_map/dot_general | solution.py:22
  100.3 0.0 copy-done.5
  100.3 0.7 copy.16
  (2 shorter events, 0.0 us)
Async XLA Ops:
  92.1 1.9 %copy-start = (bf16[4096,256]{1,0:T(8,128)(2,1)S(1)}, bf16[4096,256]{1,0:T(8,128)(2,1)}, u32[]{:S(2)}) copy-start(bf16[4096,256]{1,0:T(8,128)(2,1)} %vm_ref.1) | copy-start | bytes 6291460
  94.0 1.5 %copy-start.6 = (bf16[128,512]{1,0:T(8,128)(2,1)S(1)}, bf16[128,512]{1,0:T(8,128)(2,1)}, u32[]{:S(2)}) copy-start(bf16[128,512]{1,0:T(8,128)(2,1)} %get-tuple-element.12) | copy-start | bytes 393220
  94.0 1.4 %copy-start.3 = (bf16[2048,256]{1,0:T(8,128)(2,1)S(1)}, bf16[2048,256]{1,0:T(8,128)(2,1)}, u32[]{:S(2)}) copy-start(bf16[2048,256]{1,0:T(8,128)(2,1)} %get-tuple-element.13) | copy-start | bytes 3145732
  95.4 1.2 %copy-start.4 = (bf16[2048,256]{1,0:T(8,128)(2,1)S(1)}, bf16[2048,256]{1,0:T(8,128)(2,1)}, u32[]{:S(2)}) copy-start(bf16[2048,256]{1,0:T(8,128)(2,1)} %get-tuple-element.14) | copy-start | bytes 3145732
  95.5 2.5 %copy-start.2 = (bf16[2048,512]{1,0:T(8,128)(2,1)S(1)}, bf16[2048,512]{1,0:T(8,128)(2,1)}, u32[]{:S(2)}) copy-start(bf16[2048,512]{1,0:T(8,128)(2,1)} %get-tuple-element.11) | copy-start | bytes 6291460
  95.9 2.0 %copy-start.1 = (bf16[2048,256]{1,0:T(8,128)(2,1)S(1)}, bf16[2048,256]{1,0:T(8,128)(2,1)}, u32[]{:S(2)}) copy-start(bf16[2048,256]{1,0:T(8,128)(2,1)} %get-tuple-element.15) | copy-start | bytes 3145732
  97.9 2.4 %copy-start.5 = (bf16[128,1024]{1,0:T(8,128)(2,1)S(1)}, bf16[128,1024]{1,0:T(8,128)(2,1)}, u32[]{:S(2)}) copy-start(bf16[128,1024]{1,0:T(8,128)(2,1)} %get-tuple-element.20) | copy-start | bytes 786436
